TPU v7x, 32 devices: a whole 2x2x4 slice. The times are simulated.
32 devices in a mesh: layer: 4 (over y, x), row: 2 (over core), col: 4 (over z).
Axes of the slice: x: 2, y: 2, z: 4, core: 2. Of those that a mesh axis runs over, the one named last changes fastest.
Arguments:
- hidden: bfloat16 [384, 2304], P(('layer', 'row')), may hold values from -60 to 60
- embedding: bfloat16 [16384, 2304], P(('row', 'col'), 'layer'), may hold values from -0.3 to 0.3
- teacher: bfloat16 [384, 16384], P('layer', ('row', 'col')), may hold values from -80 to 240
Outputs:
- grad_embedding: float32 [16384, 2304], P(('row', 'col'), 'layer')
- grad_hidden: float32 [384, 2304], P(('layer', 'row', 'col'))
All inputs are finite; a program needn't handle non-finite values.
Results may differ from a plain program's by a relative error of at most 0.0041.
Values may be sent and summed in bfloat16 or wider, within the bound.
A program may use at most 192 MiB of HBM per device.

v0:
```python
import jax
import jax.numpy as jnp
from jax import lax
from jax.sharding import PartitionSpec as P

LOSS_SCALE = 256


def local(hidden, embedding, teacher):
    token_rows = lax.all_gather(hidden, "row", axis=0, tiled=True)
    width_part = lax.all_to_all(token_rows, "layer", split_axis=1, concat_axis=0, tiled=True)
    logits = lax.psum_scatter(
        lax.dot_general(
            width_part, embedding, (((1,), (1,)), ((), ())), preferred_element_type=jnp.float32
        ),
        "layer",
        scatter_dimension=0,
        tiled=True,
    )
    teach_f = teacher.astype(jnp.float32)
    top_s, top_t = lax.pmax((jnp.max(logits, axis=1), jnp.max(teach_f, axis=1)), ("row", "col"))
    part_s = jnp.sum(jnp.exp(logits - top_s[:, None]), axis=1)
    part_t = jnp.sum(jnp.exp(teach_f - top_t[:, None]), axis=1)
    sum_s, sum_t = lax.psum((part_s, part_t), ("row", "col"))
    lse_s = top_s + jnp.log(sum_s)
    lse_t = top_t + jnp.log(sum_t)
    prob_s = jnp.exp(logits - lse_s[:, None])
    prob_t = jnp.exp(teach_f - lse_t[:, None])
    grads = ((prob_s - prob_t) * LOSS_SCALE).astype(jnp.bfloat16)
    grad_piece = lax.all_gather(grads, "layer", axis=0, tiled=True)
    embed_acc = lax.dot_general(
        grad_piece, width_part, (((0,), (0,)), ((), ())), preferred_element_type=jnp.float32
    )
    hidden_piece = jnp.dot(grad_piece, embedding, preferred_element_type=jnp.float32)
    hidden_terms = lax.all_to_all(hidden_piece, "layer", split_axis=0, concat_axis=1, tiled=True)
    grad_hidden = lax.psum_scatter(hidden_terms, ("row", "col"), scatter_dimension=0, tiled=True)
    return (embed_acc, grad_hidden)


def solution(mesh):
    placed = (P(("layer", "row"), None), P(("row", "col"), "layer"), P("layer", ("row", "col")))
    return jax.shard_map(
        local,
        mesh=mesh,
        in_specs=placed,
        out_specs=(P(("row", "col"), "layer"), P(("layer", "row", "col"), None)),
        check_vma=False,
    )
```

profile of v0, /device:TPU:1, one launch (start us, length us, event | category | flops | bytes accessed | tf_op | source)
XLA Modules:
  0.0 216.0 jit_solution(10763876937868347929)
XLA Ops:
  7.2 0.0 copy-start
  7.2 0.0 reduce-scatter.4.cloned.1.call-start
  7.2 2.5 %all_gather.6 = bf16[96,2304]{1,0:T(8,128)(2,1)S(1)} all-gather(bf16[48,2304]{1,0:T(8,128)(2,1)} %param.3), channel_id=1, replica_groups=mesh['layer'=4,'row'=2,'col'=4] {'row'}, dimensions={0}, use_global_device_ids=true | all-gather | bytes 663552 | tf_op jit(solution)/shard_map/all_gather | solution.py:10
  9.7 0.6 all_to_all.28
  10.3 0.1 copy.11
  10.3 11.5 %all_to_all.38 = bf16[96,4,576]{2,0,1:T(8,128)(2,1)S(1)} all-to-all(bf16[96,4,576]{2,0,1:T(8,128)(2,1)S(1)} %copy.11), channel_id=1, replica_groups=mesh['layer'=4,'row'=2,'col'=4] {'layer'}, dimensions={1} | all-to-all | bytes 884736 | tf_op jit(solution)/shard_map/all_to_all | solution.py:11
  21.8 0.0 copy-start.2
  21.8 0.8 copy-done.2
  22.6 0.0 copy-done
  22.6 3.1 %fusion.7 = f32[384,2048]{1,0:T(8,128)} fusion(bf16[384,576]{1,0:T(8,128)(2,1)S(1)} %bitcast.14, bf16[2048,576]{0,1:T(8,128)(2,1)S(1)} %copy-done), kind=kOutput, calls=%fused_computation.12 | convolution fusion | flops 905969664 | bytes 5947392 | tf_op jit(solution)/shard_map/dot_general | solution.py:13
  25.7 0.0 copy-start.5
  25.7 0.0 reduce-scatter.4.cloned.1.call-update
  25.7 0.0 all-gather.2.cloned.1.call-start
  25.8 0.9 copy-done.5
  26.7 0.2 reduce_max.24
  26.8 43.8 %reduce-scatter.4.cloned.1.call-done = f32[96,2048]{1,0:T(8,128)} async-done(((f32[384,2048]{1,0:T(8,128)}), f32[96,2048]{1,0:T(8,128)}) %reduce-scatter.4.cloned.1.call-update) | async-done | bytes 786448 | tf_op jit(solution)/shard_map/reduce_scatter | solution.py:12
  70.6 0.0 copy-start.1
  70.6 1.3 reduce_max.23
  72.0 17.8 %all-reduce.3 = (f32[96]{0:T(128)S(1)}, f32[96]{0:T(128)S(1)}) all-reduce(bf16[96]{0:T(256)(128)(2,1)S(1)} %reduce_max.24, f32[96]{0:T(128)S(1)} %reduce_max.23), channel_id=1, replica_groups=mesh['layer'=4,'row'=2,'col'=4] {'row','col'}, use_global_device_ids=true, to_apply=%region_6.0 | all-reduce | flops 192 | bytes 1344 | tf_op jit(solution)/shard_map/pmax | solution.py:21
  89.8 1.5 fusion.2
  91.4 14.2 %all-reduce.2 = (f32[96]{0:T(128)}, f32[96]{0:T(128)}) all-reduce(f32[96]{0:T(128)S(1)} %get-tuple-element.6, f32[96]{0:T(128)S(1)} %get-tuple-element.7), channel_id=1, replica_groups=mesh['layer'=4,'row'=2,'col'=4] {'row','col'}, use_global_device_ids=true, to_apply=%region_8.0 | all-reduce | flops 192 | bytes 1536 | tf_op jit(solution)/shard_map/psum | solution.py:24
  105.6 0.7 log_add_fusion
  106.2 0.7 log_add_fusion.1
  106.9 0.0 copy-done.1
  106.9 1.1 fusion.6
  108.0 0.0 all-gather.2.cloned.1.call-update
  108.0 0.0 copy-start.6
  108.0 29.8 %all-gather.2.cloned.1.call-done = bf16[384,2048]{1,0:T(8,128)(2,1)} async-done(((bf16[96,2048]{1,0:T(8,128)(2,1)}), bf16[384,2048]{1,0:T(8,128)(2,1)}) %all-gather.2.cloned.1.call-update) | async-done | bytes 1572880 | tf_op jit(solution)/shard_map/all_gather | solution.py:30
  137.8 3.8 %fusion.9 = f32[384,576]{1,0:T(8,128)} fusion(bf16[384,2048]{1,0:T(8,128)(2,1)} %all-gather.2.cloned.1.call-done, bf16[2048,576]{0,1:T(8,128)(2,1)S(1)} %copy-done), kind=kOutput, calls=%fused_computation.14 | convolution fusion | flops 905969664 | bytes 4816896 | tf_op jit(solution)/shard_map/dot_general | solution.py:34
  141.6 3.5 %all-to-all-start.1 = ((f32[4,96,576]{2,1,0:T(8,128)}), f32[4,96,576]{2,1,0:T(8,128)S(1)}, u32[]{:S(2)}, u32[]{:S(2)}) async-start(f32[4,96,576]{2,1,0:T(8,128)} %bitcast.17), calls=%async_computation.2 | async-start | bytes 1966080 | tf_op jit(solution)/shard_map/all_to_all | solution.py:35
  145.1 0.0 copy-done.6
  145.1 0.6 dynamic-slice.4
  146.3 11.2 %all-to-all-done.1 = f32[4,96,576]{2,1,0:T(8,128)S(1)} async-done(((f32[4,96,576]{2,1,0:T(8,128)}), f32[4,96,576]{2,1,0:T(8,128)S(1)}, u32[]{:S(2)}, u32[]{:S(2)}) %all-to-all-start.1) | async-done | bytes 884768 | tf_op jit(solution)/shard_map/all_to_all | solution.py:35
  157.5 0.0 copy-start.4
  157.5 0.9 copy-done.4
  158.4 0.0 copy-start.3
  158.4 2.8 %copy.13 = f32[96,4,576]{2,1,0:T(4,128)} copy(f32[96,4,576]{2,0,1:T(8,128)} %bitcast.16) | data formatting | bytes 1769472 | tf_op jit(solution)/shard_map/all_to_all | solution.py:35
  161.3 2.7 %all_to_all.35 = f32[96,2304]{1,0:T(8,128)} reshape(f32[96,4,576]{2,1,0:T(4,128)} %copy.13) | data formatting | bytes 1769472 | tf_op jit(solution)/shard_map/all_to_all | solution.py:35
  164.0 32.7 %fusion = f32[16,2304]{1,0:T(8,128)S(1)} fusion(f32[96,2304]{1,0:T(8,128)} %all_to_all.35), kind=kCustom, calls=%all-reduce-scatter | all-reduce-scatter fusion | flops 294913 | bytes 1032704
  196.7 1.9 collective-permute-start
  198.6 2.4 %collective-permute-start.1 = (f32[12,2304]{1,0:T(8,128)S(1)}, f32[12,2304]{1,0:T(8,128)S(1)}, u32[]{:S(2)}, u32[]{:S(2)}) collective-permute-start(f32[12,2304]{1,0:T(8,128)S(1)} %slice), channel_id=1, source_target_pairs={{0,2},{1,3},{2,4},{3,5},{4,6},{5,7},{8,10},{9,11},{10,12},{11,13},... | collective-permute-start | bytes 331784
  201.0 0.0 copy-done.3
  201.0 5.0 %fusion.8 = f32[2048,576]{0,1:T(8,128)} fusion(bf16[384,2048]{1,0:T(8,128)(2,1)} %all-gather.2.cloned.1.call-done, bf16[384,576]{1,0:T(8,128)(2,1)S(1)} %bitcast.15), kind=kOutput, calls=%fused_computation.13 | convolution fusion | flops 905969664 | bytes 6733824 | tf_op jit(solution)/shard_map/dot_general | solution.py:31
  206.1 2.0 collective-permute-done.1
  208.1 0.0 collective-permute-done
  208.1 0.4 concatenate
  208.5 0.7 constant_dynamic-slice_fusion
  (1 shorter events, 0.0 us)
Async XLA Ops:
  7.2 15.5 %copy-start = (bf16[2048,576]{0,1:T(8,128)(2,1)S(1)}, bf16[2048,576]{0,1:T(8,128)(2,1)}, u32[]{:S(2)}) copy-start(bf16[2048,576]{0,1:T(8,128)(2,1)} %param.4) | copy-start | bytes 7077892
  7.2 63.5 %reduce-scatter.4.cloned.1.call-start = ((), (), s32[]{:S(2)}) async-start(), calls=%async_computation.3 | async-start | bytes 3932160 | tf_op jit(solution)/shard_map/reduce_scatter | solution.py:12
  21.8 0.8 copy-start.2
  25.7 1.0 copy-start.5
  25.7 112.1 %all-gather.2.cloned.1.call-start = ((), (), s32[]{:S(2)}) async-start(), calls=%async_computation.4 | async-start | bytes 1966080 | tf_op jit(solution)/shard_map/all_gather | solution.py:30
  70.6 36.2 %copy-start.1 = (f32[96,2048]{1,0:T(8,128)S(1)}, f32[96,2048]{1,0:T(8,128)}, u32[]{:S(2)}) copy-start(f32[96,2048]{1,0:T(8,128)} %reduce-scatter.4.cloned.1.call-done) | copy-start | bytes 2359300
  108.0 37.1 %copy-start.6 = (u32[32]{0:T(128)S(1)}, u32[32]{0:T(128)}, u32[]{:S(2)}) copy-start(u32[32]{0:T(128)} %constant.10) | copy-start | bytes 388
  141.6 15.9 %all-to-all-start.1 = ((f32[4,96,576]{2,1,0:T(8,128)}), f32[4,96,576]{2,1,0:T(8,128)S(1)}, u32[]{:S(2)}, u32[]{:S(2)}) async-start(f32[4,96,576]{2,1,0:T(8,128)} %bitcast.17), calls=%async_computation.2 | async-start | bytes 1966080 | tf_op jit(solution)/shard_map/all_to_all | solution.py:35
  157.5 0.9 copy-start.4
  158.4 42.6 %copy-start.3 = (bf16[96,4,576]{2,0,1:T(8,128)(2,1)S(1)}, bf16[96,4,576]{2,0,1:T(8,128)(2,1)}, u32[]{:S(2)}) copy-start(bf16[96,4,576]{2,0,1:T(8,128)(2,1)} %copy-done.2) | copy-start | bytes 1327108
  196.7 11.4 %collective-permute-start = (f32[16,2304]{1,0:T(8,128)S(1)}, f32[16,2304]{1,0:T(8,128)S(1)}, u32[]{:S(2)}, u32[]{:S(2)}) collective-permute-start(f32[16,2304]{1,0:T(8,128)S(1)} %fusion), channel_id=1, source_target_pairs={{0,1},{1,2},{2,3},{3,4},{4,5},{5,6},{6,7},{8,9},{9,10},{10,11},{11... | collective-permute-start | bytes 442376
  198.6 9.5 %collective-permute-start.1 = (f32[12,2304]{1,0:T(8,128)S(1)}, f32[12,2304]{1,0:T(8,128)S(1)}, u32[]{:S(2)}, u32[]{:S(2)}) collective-permute-start(f32[12,2304]{1,0:T(8,128)S(1)} %slice), channel_id=1, source_target_pairs={{0,2},{1,3},{2,4},{3,5},{4,6},{5,7},{8,10},{9,11},{10,12},{11,13},... | collective-permute-start | bytes 331784
Sparse Core Ops, SparseCore 0:
  25.8 44.7 reduce-scatter.3
  108.1 29.6 all-gather.1
where the time goes:
time: 217 us; the launch traced here: 216 us
  waiting for transfers between devices  86.8 us (40%)
  blocking collectives  78.7 us (36%)
  between operations  14.8 us (7%)
  matrix products  11.9 us (5%)
  local copies, waits for them, and re-layouts  10.5 us (5%)
  starting transfers between devices  7.91 us (4%)
  other arithmetic  5.41 us (2%)
    reduce_scatter x1, waiting for transfers between devices, local(): lax.psum_scatter(lax.dot_general(width_part, embedding, (((1,), (1,)), ((...  43.8 us
    unnamed x1, blocking collectives  32.7 us
    all_gather x1, waiting for transfers between devices, local(): grad_piece = lax.all_gather(grads, 'layer', axis=0, tiled=True)  29.8 us
    pmax x1, blocking collectives, local(): lax.pmax((jnp.max(logits, axis=1), jnp.max(teach_f, axis=1)), ('row', 'co...  17.8 us
    psum x1, blocking collectives, local(): sum_s, sum_t = lax.psum((part_s, part_t), ('row', 'col'))  14.2 us
    all_to_all x1, blocking collectives, local(): lax.all_to_all(token_rows, 'layer', split_axis=1, concat_axis=0, tiled=True)  11.5 us
    all_to_all x1, waiting for transfers between devices, local(): lax.all_to_all(hidden_piece, 'layer', split_axis=0, concat_axis=1, tiled=...  11.2 us
    all_to_all x2, local copies, waits for them, and re-layouts, local(): lax.all_to_all(hidden_piece, 'layer', split_axis=0, concat_axis=1, tiled=...  5.53 us
  transfers between devices with their start and end apart: 5, of which 4 were waited for; matrix products, arithmetic and copies ran while one was open for 3% of the time, Pallas kernels for 0%

commit v1 on v0

--- a/solution.py
+++ b/solution.py
@@ -32,7 +32,15 @@
         grad_piece, width_part, (((0,), (0,)), ((), ())), preferred_element_type=jnp.float32
     )
     hidden_piece = jnp.dot(grad_piece, embedding, preferred_element_type=jnp.float32)
-    hidden_terms = lax.all_to_all(hidden_piece, "layer", split_axis=0, concat_axis=1, tiled=True)
+    hidden_terms = jnp.concatenate(
+        lax.all_to_all(
+            jnp.stack(jnp.split(hidden_piece, lax.axis_size("layer"), axis=0)),
+            axis_name="layer",
+            split_axis=0,
+            concat_axis=0,
+        ),
+        axis=1,
+    )
     grad_hidden = lax.psum_scatter(hidden_terms, ("row", "col"), scatter_dimension=0, tiled=True)
     return (embed_acc, grad_hidden)
 

time: 217 us -> 215 us (level)
    all_to_all x2 -> x0, local copies, waits for them, and re-layouts: 5.53 us -> none  [local(): lax.all_to_all(hidden_piece, 'layer', split_axis=0, concat_axis=1, tiled=...]
    reshape x0 -> x2, local copies, waits for them, and re-layouts: none -> 4.37 us  [local(): jnp.concatenate(lax.all_to_all(jnp.stack(jnp.split(hidden_piece, lax.axis...]
where the time goes in v1:
time: 215 us
  waiting for transfers between devices  86.9 us (40%)
  blocking collectives  78.7 us (37%)
  between operations  14.8 us (7%)
  matrix products  10.9 us (5%)
  local copies, waits for them, and re-layouts  10 us (5%)
  starting transfers between devices  7.91 us (4%)
  other arithmetic  5.49 us (3%)
    reduce_scatter x1, waiting for transfers between devices, local(): lax.psum_scatter(lax.dot_general(width_part, embedding, (((1,), (1,)), ((...  43.8 us
    unnamed x1, blocking collectives  32.7 us
    all_gather x1, waiting for transfers between devices, local(): grad_piece = lax.all_gather(grads, 'layer', axis=0, tiled=True)  29.8 us
    pmax x1, blocking collectives, local(): lax.pmax((jnp.max(logits, axis=1), jnp.max(teach_f, axis=1)), ('row', 'co...  17.8 us
    psum x1, blocking collectives, local(): sum_s, sum_t = lax.psum((part_s, part_t), ('row', 'col'))  14.2 us
    all_to_all x1, blocking collectives, local(): lax.all_to_all(token_rows, 'layer', split_axis=1, concat_axis=0, tiled=True)  11.5 us
    all_to_all x1, waiting for transfers between devices, local(): lax.all_to_all(jnp.stack(jnp.split(hidden_piece, lax.axis_size('layer'),...  11.2 us
    dot_general x1, matrix products, local(): lax.dot_general(grad_piece, width_part, (((0,), (0,)), ((), ())), preferr...  5.03 us
  transfers between devices with their start and end apart: 5, of which 4 were waited for; matrix products, arithmetic and copies ran while one was open for 3% of the time, Pallas kernels for 0%

profile of v1, /device:TPU:1, one launch (start us, length us, event | category | flops | bytes accessed | tf_op | source)
XLA Modules:
  0.0 214.7 jit_solution(13435907915188764334)
XLA Ops:
  7.2 0.0 copy-start
  7.2 0.0 reduce-scatter.4.cloned.1.call-start
  7.2 2.5 %all_gather.6 = bf16[96,2304]{1,0:T(8,128)(2,1)S(1)} all-gather(bf16[48,2304]{1,0:T(8,128)(2,1)} %param.3), channel_id=1, replica_groups=mesh['layer'=4,'row'=2,'col'=4] {'row'}, dimensions={0}, use_global_device_ids=true | all-gather | bytes 663552 | tf_op jit(solution)/shard_map/all_gather | solution.py:10
  9.7 0.6 all_to_all.17
  10.3 0.1 copy.10
  10.3 11.5 %all_to_all.24 = bf16[96,4,576]{2,0,1:T(8,128)(2,1)S(1)} all-to-all(bf16[96,4,576]{2,0,1:T(8,128)(2,1)S(1)} %copy.10), channel_id=1, replica_groups=mesh['layer'=4,'row'=2,'col'=4] {'layer'}, dimensions={1} | all-to-all | bytes 884736 | tf_op jit(solution)/shard_map/all_to_all | solution.py:11
  21.8 0.0 copy-start.2
  21.8 0.8 copy-done.2
  22.6 0.0 copy-done
  22.6 3.1 %fusion.7 = f32[384,2048]{1,0:T(8,128)} fusion(bf16[384,576]{1,0:T(8,128)(2,1)S(1)} %bitcast.21, bf16[2048,576]{0,1:T(8,128)(2,1)S(1)} %copy-done), kind=kOutput, calls=%fused_computation.17 | convolution fusion | flops 905969664 | bytes 5947392 | tf_op jit(solution)/shard_map/dot_general | solution.py:13
  25.7 0.0 copy-start.4
  25.7 0.0 reduce-scatter.4.cloned.1.call-update
  25.7 0.0 all-gather.2.cloned.1.call-start
  25.8 0.9 copy-done.4
  26.7 0.2 reduce_max.24
  26.8 43.8 %reduce-scatter.4.cloned.1.call-done = f32[96,2048]{1,0:T(8,128)} async-done(((f32[384,2048]{1,0:T(8,128)}), f32[96,2048]{1,0:T(8,128)}) %reduce-scatter.4.cloned.1.call-update) | async-done | bytes 786448 | tf_op jit(solution)/shard_map/reduce_scatter | solution.py:12
  70.6 0.0 copy-start.1
  70.6 1.3 reduce_max.23
  72.0 17.8 %all-reduce.3 = (f32[96]{0:T(128)S(1)}, f32[96]{0:T(128)S(1)}) all-reduce(bf16[96]{0:T(256)(128)(2,1)S(1)} %reduce_max.24, f32[96]{0:T(128)S(1)} %reduce_max.23), channel_id=1, replica_groups=mesh['layer'=4,'row'=2,'col'=4] {'row','col'}, use_global_device_ids=true, to_apply=%region_6.0 | all-reduce | flops 192 | bytes 1344 | tf_op jit(solution)/shard_map/pmax | solution.py:21
  89.8 1.5 fusion.2
  91.4 14.2 %all-reduce.2 = (f32[96]{0:T(128)}, f32[96]{0:T(128)}) all-reduce(f32[96]{0:T(128)S(1)} %get-tuple-element.10, f32[96]{0:T(128)S(1)} %get-tuple-element.11), channel_id=1, replica_groups=mesh['layer'=4,'row'=2,'col'=4] {'row','col'}, use_global_device_ids=true, to_apply=%region_8.0 | all-reduce | flops 192 | bytes 1536 | tf_op jit(solution)/shard_map/psum | solution.py:24
  105.6 0.7 log_add_fusion
  106.2 0.7 log_add_fusion.1
  106.9 0.0 copy-done.1
  106.9 1.1 fusion.6
  108.0 0.0 all-gather.2.cloned.1.call-update
  108.0 29.8 %all-gather.2.cloned.1.call-done = bf16[384,2048]{1,0:T(8,128)(2,1)} async-done(((bf16[96,2048]{1,0:T(8,128)(2,1)}), bf16[384,2048]{1,0:T(8,128)(2,1)}) %all-gather.2.cloned.1.call-update) | async-done | bytes 1572880 | tf_op jit(solution)/shard_map/all_gather | solution.py:30
  137.8 2.8 %fusion.9 = f32[384,576]{0,1:T(8,128)S(1)} fusion(bf16[384,2048]{1,0:T(8,128)(2,1)} %all-gather.2.cloned.1.call-done, bf16[2048,576]{0,1:T(8,128)(2,1)S(1)} %copy-done), kind=kOutput, calls=%fused_computation.19 | convolution fusion | flops 905969664 | bytes 4816896 | tf_op jit(solution)/shard_map/dot_general | solution.py:34
  140.6 0.3 slice_bitcast_fusion.3
  140.9 0.1 pad_maximum_fusion
  141.0 0.0 copy-start.5
  141.0 1.3 copy.11
  142.3 3.5 %all-to-all-start.1 = ((f32[4,96,576]{2,1,0:T(8,128)}), f32[4,96,576]{2,1,0:T(8,128)S(1)}, u32[]{:S(2)}, u32[]{:S(2)}) async-start(f32[4,96,576]{2,1,0:T(8,128)} %copy.11), calls=%async_computation.2 | async-start | bytes 1966080 | tf_op jit(solution)/shard_map/all_to_all | solution.py:36
  145.8 0.0 copy-done.5
  145.9 0.6 dynamic-slice.4
  147.1 11.2 %all-to-all-done.1 = f32[4,96,576]{2,1,0:T(8,128)S(1)} async-done(((f32[4,96,576]{2,1,0:T(8,128)}), f32[4,96,576]{2,1,0:T(8,128)S(1)}, u32[]{:S(2)}, u32[]{:S(2)}) %all-to-all-start.1) | async-done | bytes 884768 | tf_op jit(solution)/shard_map/all_to_all | solution.py:36
  158.3 1.6 copy.12
  159.8 0.0 copy-start.3
  159.8 2.8 %reshape.18 = f32[96,2304]{1,0:T(8,128)} reshape(f32[96,4,576]{2,1,0:T(4,128)} %copy.12) | data formatting | bytes 1769472 | tf_op jit(solution)/shard_map/reshape | solution.py:35
  162.6 32.7 %fusion = f32[16,2304]{1,0:T(8,128)S(1)} fusion(f32[96,2304]{1,0:T(8,128)} %reshape.18), kind=kCustom, calls=%all-reduce-scatter | all-reduce-scatter fusion | flops 294913 | bytes 1032704
  195.4 1.9 collective-permute-start
  197.3 2.4 %collective-permute-start.1 = (f32[12,2304]{1,0:T(8,128)S(1)}, f32[12,2304]{1,0:T(8,128)S(1)}, u32[]{:S(2)}, u32[]{:S(2)}) collective-permute-start(f32[12,2304]{1,0:T(8,128)S(1)} %slice), channel_id=1, source_target_pairs={{0,2},{1,3},{2,4},{3,5},{4,6},{5,7},{8,10},{9,11},{10,12},{11,13},... | collective-permute-start | bytes 331784
  199.7 0.0 copy-done.3
  199.7 5.0 %fusion.8 = f32[2048,576]{0,1:T(8,128)} fusion(bf16[384,2048]{1,0:T(8,128)(2,1)} %all-gather.2.cloned.1.call-done, bf16[384,576]{1,0:T(8,128)(2,1)S(1)} %bitcast.22), kind=kOutput, calls=%fused_computation.18 | convolution fusion | flops 905969664 | bytes 6733824 | tf_op jit(solution)/shard_map/dot_general | solution.py:31
  204.7 2.0 collective-permute-done.1
  206.8 0.0 collective-permute-done
  206.8 0.4 concatenate
  207.2 0.7 constant_dynamic-slice_fusion
  (1 shorter events, 0.0 us)
Async XLA Ops:
  7.2 15.5 %copy-start = (bf16[2048,576]{0,1:T(8,128)(2,1)S(1)}, bf16[2048,576]{0,1:T(8,128)(2,1)}, u32[]{:S(2)}) copy-start(bf16[2048,576]{0,1:T(8,128)(2,1)} %param.4) | copy-start | bytes 7077892
  7.2 63.5 %reduce-scatter.4.cloned.1.call-start = ((), (), s32[]{:S(2)}) async-start(), calls=%async_computation.3 | async-start | bytes 3932160 | tf_op jit(solution)/shard_map/reduce_scatter | solution.py:12
  21.8 0.8 copy-start.2
  25.7 1.0 copy-start.4
  25.7 112.1 %all-gather.2.cloned.1.call-start = ((), (), s32[]{:S(2)}) async-start(), calls=%async_computation.4 | async-start | bytes 1966080 | tf_op jit(solution)/shard_map/all_gather | solution.py:30
  70.6 36.2 %copy-start.1 = (f32[96,2048]{1,0:T(8,128)S(1)}, f32[96,2048]{1,0:T(8,128)}, u32[]{:S(2)}) copy-start(f32[96,2048]{1,0:T(8,128)} %reduce-scatter.4.cloned.1.call-done) | copy-start | bytes 2359300
  141.0 4.9 %copy-start.5 = (u32[32]{0:T(128)S(1)}, u32[32]{0:T(128)}, u32[]{:S(2)}) copy-start(u32[32]{0:T(128)} %constant.10) | copy-start | bytes 388
  142.3 15.9 %all-to-all-start.1 = ((f32[4,96,576]{2,1,0:T(8,128)}), f32[4,96,576]{2,1,0:T(8,128)S(1)}, u32[]{:S(2)}, u32[]{:S(2)}) async-start(f32[4,96,576]{2,1,0:T(8,128)} %copy.11), calls=%async_computation.2 | async-start | bytes 1966080 | tf_op jit(solution)/shard_map/all_to_all | solution.py:36
  159.8 39.9 %copy-start.3 = (bf16[96,4,576]{2,0,1:T(8,128)(2,1)S(1)}, bf16[96,4,576]{2,0,1:T(8,128)(2,1)}, u32[]{:S(2)}) copy-start(bf16[96,4,576]{2,0,1:T(8,128)(2,1)} %copy-done.2) | copy-start | bytes 1327108
  195.4 11.4 %collective-permute-start = (f32[16,2304]{1,0:T(8,128)S(1)}, f32[16,2304]{1,0:T(8,128)S(1)}, u32[]{:S(2)}, u32[]{:S(2)}) collective-permute-start(f32[16,2304]{1,0:T(8,128)S(1)} %fusion), channel_id=1, source_target_pairs={{0,1},{1,2},{2,3},{3,4},{4,5},{5,6},{6,7},{8,9},{9,10},{10,11},{11... | collective-permute-start | bytes 442376
  197.3 9.5 %collective-permute-start.1 = (f32[12,2304]{1,0:T(8,128)S(1)}, f32[12,2304]{1,0:T(8,128)S(1)}, u32[]{:S(2)}, u32[]{:S(2)}) collective-permute-start(f32[12,2304]{1,0:T(8,128)S(1)} %slice), channel_id=1, source_target_pairs={{0,2},{1,3},{2,4},{3,5},{4,6},{5,7},{8,10},{9,11},{10,12},{11,13},... | collective-permute-start | bytes 331784
Sparse Core Ops, SparseCore 0:
  25.8 44.7 reduce-scatter.3
  108.1 29.6 all-gather.1
